TPU v7x, 32 devices: a whole 2x2x4 slice. The times are simulated.
32 devices in a mesh: gx: 4 (over y, core), gy: 4 (over z), gz: 2 (over x).
Axes of the slice: x: 2, y: 2, z: 4, core: 2. Of those that a mesh axis runs over, the one named last changes fastest.
Arguments:
- moments: float32 [8, 16, 64, 1024], P(None, 'gx', 'gy', 'gz'), may hold values from 0.001 to 60, as said below
- velocity: float32 [3, 16, 64, 1024], P(None, 'gx', 'gy', 'gz'), may hold values from -4 to 4
- drift: float32 [3, 16, 64, 1024], P(None, 'gx', 'gy', 'gz'), may hold values from -8 to 8
Outputs:
- updated: float32 [8, 16, 64, 1024], P(None, 'gx', 'gy', 'gz')
- totals: float32 [8], replicated
Inputs may be any that keep to these rules, and one draw needn't show every extreme that they name: In every cell the 8 entries are the moments of order 0 to 7 of a log-normal distribution of particle size.
All inputs are finite; a program needn't handle non-finite values. Where the computation divides by a largest or mean magnitude, that divisor is 1e-20 or more.
Results may differ from a plain program's by a relative error of at most 0.0003.
Values sent between devices are 32-bit elements; how exact they have to be, the bound alone decides.
A program may use at most 64 MiB of HBM per device.

v0:
```python
import jax
import jax.numpy as jnp
from jax import lax
from jax.sharding import PartitionSpec as P

SWEEPS = 6
cfl_number = 0.4
speed_eps = 1e-06
pair_list = ((0, 1), (0, 2), (0, 3), (1, 2), (1, 3), (2, 3))


def padded(shard, sides, width, wrap):
    for axis, dim in sides:
        count, length = (lax.axis_size(axis), shard.shape[dim])
        up = [(i, (i + 1) % count) for i in range(count if wrap else count - 1)]
        down = [(j, i) for i, j in up]
        last = lax.slice_in_dim(shard, length - width, length, axis=dim)
        leading = lax.slice_in_dim(shard, 0, width, axis=dim)
        before = lax.ppermute(last, axis, up)
        after = lax.ppermute(leading, axis, down)
        shard = jnp.concatenate([before, shard, after], axis=dim)
    return shard


def entry_key(first_index, second_index):
    return (min(first_index, second_index), max(first_index, second_index))


def invert(moment):
    levels = [moment[order] for order in range(8)]
    zeros = jnp.zeros_like(levels[0])
    before = [zeros] * 8
    alphas = [levels[1] / levels[0]]
    betas = [levels[0]]
    for level in range(1, 4):
        fresh = [zeros] * 8
        for column in range(level, 8 - level):
            fresh[column] = (
                levels[column + 1]
                - alphas[level - 1] * levels[column]
                - betas[level - 1] * before[column]
            )
        alphas.append(fresh[level + 1] / fresh[level] - levels[level] / levels[level - 1])
        betas.append(fresh[level] / levels[level - 1])
        before, levels = (levels, fresh)
    table = {}
    for row_index in range(4):
        for col_index in range(row_index, 4):
            table[row_index, col_index] = zeros
    for row_index in range(4):
        table[row_index, row_index] = alphas[row_index]
    for row_index in range(3):
        table[row_index, row_index + 1] = jnp.sqrt(betas[row_index + 1])
    first = [jnp.ones_like(zeros), zeros, zeros, zeros]
    for _ in range(SWEEPS):
        for pivot, other in pair_list:
            coupling = table[pivot, other]
            head = table[pivot, pivot]
            tail = table[other, other]
            spread = tail - head
            orient = jnp.where(spread >= 0, 1.0, -1.0)
            tangent = (
                orient
                * 2.0
                * coupling
                / (jnp.abs(spread) + jnp.sqrt(spread * spread + 4.0 * coupling * coupling))
            )
            cosine = 1.0 / jnp.sqrt(1.0 + tangent * tangent)
            sine = tangent * cosine
            for rest in range(4):
                if rest != pivot and rest != other:
                    near = table[entry_key(rest, pivot)]
                    far = table[entry_key(rest, other)]
                    table[entry_key(rest, pivot)] = cosine * near - sine * far
                    table[entry_key(rest, other)] = sine * near + cosine * far
            table[pivot, pivot] = head - tangent * coupling
            table[other, other] = tail + tangent * coupling
            table[pivot, other] = jnp.zeros_like(coupling)
            first_p = first[pivot]
            first_q = first[other]
            first[pivot] = cosine * first_p - sine * first_q
            first[other] = sine * first_p + cosine * first_q
    weights = [moment[0] * first[node] * first[node] for node in range(4)]
    places = [table[node, node] for node in range(4)]
    return jnp.stack(weights + places)


def face_flux(extended, axis, count):

    def part(channel, start):
        return lax.slice_in_dim(extended[channel], start, start + count + 1, axis=axis - 1)

    mean_speed = 0.5 * (part(8, 0) + part(8, 1))
    mean_drift = 0.5 * (part(9, 0) + part(9, 1))
    zeros = jnp.zeros_like(mean_speed)
    accum = [zeros] * 8
    for node in range(4):
        for start, upwind in ((0, jnp.maximum), (1, jnp.minimum)):
            size = part(4 + node, start)
            carried = part(node, start) * upwind(mean_speed + mean_drift * size, 0.0)
            for order in range(8):
                accum[order] = accum[order] + carried
                carried = carried * size
    return jnp.stack(accum)


def shards(moments, velocity, drift):
    counts = moments.shape
    cells_total = (
        counts[1]
        * lax.axis_size("gx")
        * counts[2]
        * lax.axis_size("gy")
        * counts[3]
        * lax.axis_size("gz")
    )
    bottom = lax.axis_index("gz") == 0
    top = lax.axis_index("gz") == lax.axis_size("gz") - 1
    nodes = invert(moments)
    packs = [
        jnp.concatenate(
            [nodes, velocity[direction : direction + 1], drift[direction : direction + 1]], 0
        )
        for direction in range(3)
    ]
    extended_x = padded(packs[0], (("gx", 1),), 1, True)
    extended_y = padded(packs[1], (("gy", 2),), 1, True)
    extended_z = padded(packs[2], (("gz", 3),), 1, False)
    change = jnp.zeros_like(moments)
    for direction, extended in ((0, extended_x), (1, extended_y), (2, extended_z)):
        axis = direction + 1
        count = counts[axis]
        flux = face_flux(extended, axis, count)
        if direction == 2:
            face = lax.broadcasted_iota(jnp.int32, flux.shape, 3)
            wall = (face == 0) & bottom | (face == count) & top
            flux = jnp.where(wall, 0.0, flux)
        change = (
            change
            + lax.slice_in_dim(flux, 1, count + 1, axis=axis)
            - lax.slice_in_dim(flux, 0, count, axis=axis)
        )
    speed = jnp.zeros_like(moments[0])
    for direction in range(3):
        speed = speed + jnp.max(
            jnp.abs(velocity[direction][None] + drift[direction][None] * nodes[4:8]), axis=0
        )
    local_max = jnp.max(speed)
    global_max = lax.pmax(local_max, ("gx", "gy", "gz"))
    step_size = cfl_number / (global_max + speed_eps)
    updated = moments - step_size * change
    sums = lax.psum(jnp.sum(updated, axis=(1, 2, 3)), ("gx", "gy", "gz"))
    totals = sums / cells_total
    return (updated, totals)


def solution(mesh):
    in_specs = (P(None, "gx", "gy", "gz"), P(None, "gx", "gy", "gz"), P(None, "gx", "gy", "gz"))
    out_specs = (P(None, "gx", "gy", "gz"), P())
    return jax.shard_map(shards, mesh=mesh, in_specs=in_specs, out_specs=out_specs, check_vma=False)
```

profile of v0, /device:TPU:10, one launch (start us, length us, event | category | flops | bytes accessed | tf_op | source)
XLA Modules:
  0.0 132.4 jit_solution(10353812203924966196)
XLA Ops:
  0.6 1.1 subtract_subtract_fusion.4
  1.8 1.5 %divide_sqrt_fusion = (f32[1,4,16,512]{3,2,1,0:T(8,128)S(1)}, f32[1,4,16,512]{3,2,1,0:T(8,128)S(1)}, f32[1,4,16,512]{3,2,1,0:T(8,128)S(1)}, f32[1,4,16,512]{3,2,...) fusion(f32[8,4,16,512]{3,2,1,0:T(8,128)} %param.3, ...), kind=kLoop, calls=%fused_computation.610 | loop fusion | flops 1179648 | bytes 2228224 | tf_op jit(solution)/shard_map/sqrt | solution.py:53
  3.5 1.1 multiply_add_fusion.28
  4.6 0.4 multiply_subtract_fusion.86
  5.0 0.5 multiply_add_fusion.83
  5.5 0.9 multiply_add_fusion.23
  6.4 0.3 multiply_add_fusion.76
  6.7 0.3 fusion.211
  7.1 1.1 multiply_add_fusion.16
  8.2 0.8 multiply_subtract_fusion.105
  9.2 0.8 multiply_add_fusion.11
  10.0 0.3 multiply_subtract_fusion.50
  10.3 0.8 multiply_add_fusion.44
  11.1 1.1 multiply_add_fusion.36
  12.1 0.3 multiply_add_fusion.4
  12.5 0.3 fusion.171
  12.8 0.6 multiply_multiply_fusion
  13.8 0.7 constant_dynamic-update-slice_fusion.18
  14.4 0.7 constant_dynamic-update-slice_fusion.17
  15.5 0.8 copy-done.4
  16.4 0.7 slice_bitcast_fusion.25
  17.1 0.3 copy-done.5
  17.4 0.8 slice_bitcast_fusion.24
  18.2 0.9 fusion.284
  19.1 1.7 %collective-permute-start.1 = (f32[10,1,16,512]{3,2,1,0:T(8,128)}, f32[10,1,16,512]{3,2,1,0:T(8,128)S(1)}, u32[]{:S(2)}, u32[]{:S(2)}) collective-permute-start(f32[10,1,16,512]{3,2,1,0:T(8,128)} %get-tuple-element.278), channel_id=1, source_target_pairs={{8,0},{16,8},{24,16},{0,24},{9,1},{17,9},{25,17},{1,25},{10,2},{18... | collective-permute-start | bytes 983048 | tf_op jit(solution)/shard_map/ppermute | solution.py:20
  20.9 0.8 fusion.285
  21.6 0.7 copy.31
  22.3 1.6 %collective-permute-start.2 = (f32[10,4,1,512]{3,0,2,1:T(8,128)}, f32[10,4,1,512]{3,0,2,1:T(8,128)}, u32[]{:S(2)}, u32[]{:S(2)}) collective-permute-start(f32[10,4,1,512]{3,0,2,1:T(8,128)} %copy.31), channel_id=1, source_target_pairs={{0,2},{2,4},{4,6},{6,0},{1,3},{3,5},{5,7},{7,1},{8,10},{10,12},{12... | collective-permute-start | bytes 245768 | tf_op jit(solution)/shard_map/ppermute | solution.py:19
  23.9 0.9 fusion.286
  24.9 1.3 collective-permute-start.4
  26.1 6.0 %collective-permute-start.5 = (f32[10,4,16,1]{3,2,1,0:T(8,128)}, f32[10,4,16,1]{3,2,1,0:T(8,128)}, u32[]{:S(2)}, u32[]{:S(2)}) collective-permute-start(f32[10,4,16,1]{3,2,1,0:T(8,128)} %get-tuple-element.282), channel_id=1, source_target_pairs={{1,0},{3,2},{5,4},{7,6},{9,8},{11,10},{13,12},{15,14},{17,16},{19,... | collective-permute-start | bytes 7688 | tf_op jit(solution)/shard_map/ppermute | solution.py:20
  32.1 1.4 %abs_reduce_fusion.1 = (f32[4,16,512]{2,1,0:T(8,128)S(1)}, f32[4,16,512]{2,1,0:T(8,128)S(1)}, f32[4,16,512]{2,1,0:T(8,128)S(1)}) fusion(f32[4,16,512]{2,1,0:T(8,128)} %get-tuple-element.293, f32[4,16,512]{2,1,0:T(8,128)} %get-tuple-element.287, f32[1,4,16,512]{3,2,1,0:T(8,128)S(1)} %get-tuple-element.61, f32[1,4,16,512]{3,2,1,0:T(8,128)} %get-tuple-element.63, ...), kind=kLoop, calls=%fused_computation.48 | loop fusion | flops 1867776 | bytes 1703936 | tf_op jit(solution)/shard_map/reduce_max | solution.py:145
  33.6 0.6 add_reduce_fusion
  34.2 40.1 %pmax.7 = f32[]{:T(128)} all-reduce(f32[]{:T(128)} %add_reduce_fusion), channel_id=1, replica_groups=mesh['gx'=4,'gy'=4,'gz'=2] {'gx','gy','gz'}, use_global_device_ids=true, to_apply=%region_4.5 | all-reduce | flops 1 | bytes 8 | tf_op jit(solution)/shard_map/pmax | solution.py:149
  74.3 0.9 copy.32
  75.9 1.8 %collective-permute-start.3 = (f32[10,4,1,512]{3,0,2,1:T(8,128)S(1)}, f32[10,4,1,512]{3,0,2,1:T(8,128)S(1)}, u32[]{:S(2)}, u32[]{:S(2)}) collective-permute-start(f32[10,4,1,512]{3,0,2,1:T(8,128)S(1)} %copy.32), channel_id=1, source_target_pairs={{2,0},{4,2},{6,4},{0,6},{3,1},{5,3},{7,5},{1,7},{10,8},{12,10},{14... | collective-permute-start | bytes 245768 | tf_op jit(solution)/shard_map/ppermute | solution.py:20
  77.7 2.0 %pad_maximum_fusion.1 = f32[10,4,16,514]{3,2,1,0:T(8,128)S(1)} fusion(f32[10,4,16,1]{3,2,1,0:T(8,128)} %collective-permute-done.5, f32[10,4,16,512]{3,2,1,0:T(8,128)} %copy-done.1, f32[10,4,16,1]{3,2,1,0:T(8,128)} %collective-permute-done.4), kind=kLoop, calls=%fused_computation.37 | loop fusion | flops 657920 | bytes 2631680 | tf_op jit(solution)/shard_map/concatenate | solution.py:21
  79.9 0.5 bitcast_dynamic-update-slice_fusion.15
  80.6 0.2 bitcast_dynamic-update-slice_fusion.13
  80.9 0.3 bitcast_dynamic-update-slice_fusion.12
  81.4 0.2 bitcast_dynamic-update-slice_fusion.10
  81.7 0.2 bitcast_dynamic-update-slice_fusion.9
  81.9 0.3 bitcast_dynamic-update-slice_fusion.8
  82.4 1.1 copy.33
  83.6 0.4 pad_maximum_fusion
  84.2 0.5 bitcast_dynamic-update-slice_fusion.7
  84.7 0.3 bitcast_dynamic-update-slice_fusion.6
  84.9 0.3 bitcast_dynamic-update-slice_fusion.5
  85.2 0.3 bitcast_dynamic-update-slice_fusion.4
  85.6 0.3 bitcast_dynamic-update-slice_fusion.3
  85.8 0.3 bitcast_dynamic-update-slice_fusion.2
  86.1 0.3 bitcast_dynamic-update-slice_fusion.1
  86.5 0.3 bitcast_dynamic-update-slice_fusion
  86.9 0.3 add_dynamic-update-slice_fusion.7
  87.2 0.3 add_dynamic-update-slice_fusion.6
  87.5 0.3 add_dynamic-update-slice_fusion.5
  87.8 0.3 add_dynamic-update-slice_fusion.4
  88.1 0.3 add_dynamic-update-slice_fusion.3
  88.4 0.3 add_dynamic-update-slice_fusion.2
  88.8 0.3 add_dynamic-update-slice_fusion.1
  89.1 0.3 add_dynamic-update-slice_fusion
  89.5 1.6 %fusion.223 = (f32[8]{0:T(128)S(1)}, f32[8,4,16,512]{3,2,1,0:T(8,128)}) fusion(f32[8,4,16,512]{3,2,1,0:T(8,128)S(1)} %copy-done, f32[8,4,16,513]{3,2,1,0:T(8,128)S(1)} %broadcast_select_fusion, f32[8,4,17,512]{3,2,1,0:T(8,128)S(1)} %bitcast_dynamic-update-slice_fusion, f32[8,5,16,512]{3,2,1,0:T(8,128)S(1)} %add_dynamic-update-slice_fusion, f32[]{:T(128)S(6)} %div.553), kind=kLoop, calls=%fused_computation.747 | loop fusion | flops 2097144 | bytes 8388644 | tf_op jit(solution)/shard_map/reduce_sum | solution.py:152
  91.1 40.8 %psum.7 = f32[8]{0:T(128)S(1)} all-reduce(f32[8]{0:T(128)S(1)} %get-tuple-element.5), channel_id=1, replica_groups=mesh['gx'=4,'gy'=4,'gz'=2] {'gx','gy','gz'}, use_global_device_ids=true, to_apply=%region_6.7 | all-reduce | flops 8 | bytes 64 | tf_op jit(solution)/shard_map/psum | solution.py:152
  131.9 0.5 broadcast_multiply_fusion
  (38 shorter events, 2.2 us)
Async XLA Ops:
  1.8 1.7 %copy-start = (f32[8,4,16,512]{3,2,1,0:T(8,128)S(1)}, f32[8,4,16,512]{3,2,1,0:T(8,128)}, u32[]{:S(2)}) copy-start(f32[8,4,16,512]{3,2,1,0:T(8,128)} %param.3) | copy-start | bytes 3145732
  15.4 1.0 copy-start.4
  16.4 1.0 copy-start.5
  18.2 5.8 %copy-start.1 = (f32[10,4,16,512]{3,2,1,0:T(8,128)}, f32[10,4,16,512]{3,2,1,0:T(8,128)S(1)}, u32[]{:S(2)}) copy-start(f32[10,4,16,512]{3,2,1,0:T(8,128)S(1)} %get-tuple-element.291) | copy-start | bytes 3932164
  18.2 6.7 %copy-start.2 = (f32[10,4,16,512]{3,2,1,0:T(8,128)}, f32[10,4,16,512]{3,2,1,0:T(8,128)S(1)}, u32[]{:S(2)}) copy-start(f32[10,4,16,512]{3,2,1,0:T(8,128)S(1)} %get-tuple-element.290) | copy-start | bytes 3932164
  19.1 67.7 %collective-permute-start = (f32[10,1,16,512]{3,2,1,0:T(8,128)}, f32[10,1,16,512]{3,2,1,0:T(8,128)S(1)}, u32[]{:S(2)}, u32[]{:S(2)}) collective-permute-start(f32[10,1,16,512]{3,2,1,0:T(8,128)} %get-tuple-element.277), channel_id=1, source_target_pairs={{0,8},{8,16},{16,24},{24,0},{1,9},{9,17},{17,25},{25,1},{2,10},{10... | collective-permute-start | bytes 983048 | tf_op jit(solution)/shard_map/ppermute | solution.py:19
  19.1 67.7 %collective-permute-start.1 = (f32[10,1,16,512]{3,2,1,0:T(8,128)}, f32[10,1,16,512]{3,2,1,0:T(8,128)S(1)}, u32[]{:S(2)}, u32[]{:S(2)}) collective-permute-start(f32[10,1,16,512]{3,2,1,0:T(8,128)} %get-tuple-element.278), channel_id=1, source_target_pairs={{8,0},{16,8},{24,16},{0,24},{9,1},{17,9},{25,17},{1,25},{10,2},{18... | collective-permute-start | bytes 983048 | tf_op jit(solution)/shard_map/ppermute | solution.py:20
  22.3 60.0 %collective-permute-start.2 = (f32[10,4,1,512]{3,0,2,1:T(8,128)}, f32[10,4,1,512]{3,0,2,1:T(8,128)}, u32[]{:S(2)}, u32[]{:S(2)}) collective-permute-start(f32[10,4,1,512]{3,0,2,1:T(8,128)} %copy.31), channel_id=1, source_target_pairs={{0,2},{2,4},{4,6},{6,0},{1,3},{3,5},{5,7},{7,1},{8,10},{10,12},{12... | collective-permute-start | bytes 245768 | tf_op jit(solution)/shard_map/ppermute | solution.py:19
  24.9 51.0 %collective-permute-start.4 = (f32[10,4,16,1]{3,2,1,0:T(8,128)}, f32[10,4,16,1]{3,2,1,0:T(8,128)}, u32[]{:S(2)}, u32[]{:S(2)}) collective-permute-start(f32[10,4,16,1]{3,2,1,0:T(8,128)} %get-tuple-element.281), channel_id=1, source_target_pairs={{0,1},{2,3},{4,5},{6,7},{8,9},{10,11},{12,13},{14,15},{16,17},{18,... | collective-permute-start | bytes 7688 | tf_op jit(solution)/shard_map/ppermute | solution.py:19
  26.1 51.6 %collective-permute-start.5 = (f32[10,4,16,1]{3,2,1,0:T(8,128)}, f32[10,4,16,1]{3,2,1,0:T(8,128)}, u32[]{:S(2)}, u32[]{:S(2)}) collective-permute-start(f32[10,4,16,1]{3,2,1,0:T(8,128)} %get-tuple-element.282), channel_id=1, source_target_pairs={{1,0},{3,2},{5,4},{7,6},{9,8},{11,10},{13,12},{15,14},{17,16},{19,... | collective-permute-start | bytes 7688 | tf_op jit(solution)/shard_map/ppermute | solution.py:20
  75.9 7.6 %collective-permute-start.3 = (f32[10,4,1,512]{3,0,2,1:T(8,128)S(1)}, f32[10,4,1,512]{3,0,2,1:T(8,128)S(1)}, u32[]{:S(2)}, u32[]{:S(2)}) collective-permute-start(f32[10,4,1,512]{3,0,2,1:T(8,128)S(1)} %copy.32), channel_id=1, source_target_pairs={{2,0},{4,2},{6,4},{0,6},{3,1},{5,3},{7,5},{1,7},{10,8},{12,10},{14... | collective-permute-start | bytes 245768 | tf_op jit(solution)/shard_map/ppermute | solution.py:20
  82.2 1.4 %copy-start.3 = (f32[10,4,16,512]{3,2,1,0:T(8,128)S(1)}, f32[10,4,16,512]{3,2,1,0:T(8,128)}, u32[]{:S(2)}) copy-start(f32[10,4,16,512]{3,2,1,0:T(8,128)} %copy-done.2) | copy-start | bytes 3932164
where the time goes:
time: 133 us; the launch traced here: 132 us
  blocking collectives  80.9 us (61%)
  other arithmetic  28.5 us (21%)
  starting transfers between devices  12.4 us (9%)
  local copies, waits for them, and re-layouts  8.81 us (7%)
  between operations  1.78 us (1%)
    psum x1, blocking collectives, shards(): sums = lax.psum(jnp.sum(updated, axis=(1, 2, 3)), ('gx', 'gy', 'gz'))  40.8 us
    pmax x1, blocking collectives, shards(): global_max = lax.pmax(local_max, ('gx', 'gy', 'gz'))  40.1 us
    ppermute x3, starting transfers between devices, padded(): after = lax.ppermute(leading, axis, down)  9.56 us
    unnamed x25, other arithmetic  7.93 us
    add x5, other arithmetic, invert(): first[other] = sine * first_p + cosine * first_q  4.27 us
    slice x4, local copies, waits for them, and re-layouts, padded(): last = lax.slice_in_dim(shard, length - width, length, axis=dim)  3.34 us
    ppermute x3, starting transfers between devices, padded(): before = lax.ppermute(last, axis, up)  2.86 us
    add x5, other arithmetic, invert(): table[entry_key(rest, other)] = sine * near + cosine * far  2.86 us
  transfers between devices with their start and end apart: 6, of which 0 were waited for; matrix products, arithmetic and copies ran while one was open for 11% of the time, Pallas kernels for 0%

commit v1 on v0

--- a/solution.py
+++ b/solution.py
@@ -149,7 +149,7 @@
     global_max = lax.pmax(local_max, ("gx", "gy", "gz"))
     step_size = cfl_number / (global_max + speed_eps)
     updated = moments - step_size * change
-    sums = lax.psum(jnp.sum(updated, axis=(1, 2, 3)), ("gx", "gy", "gz"))
+    sums = jnp.sum(lax.all_gather(jnp.sum(updated, axis=(1, 2, 3)), ("gx", "gy", "gz")), axis=0)
     totals = sums / cells_total
     return (updated, totals)
 

time: 133 us -> 133 us (level)
    unnamed x0 -> x1, blocking collectives: none -> 40.9 us
    psum x1 -> x0, blocking collectives: 40.8 us -> none  [shards(): sums = lax.psum(jnp.sum(updated, axis=(1, 2, 3)), ('gx', 'gy', 'gz'))]
where the time goes in v1:
time: 133 us
  blocking collectives  80.9 us (61%)
  other arithmetic  28.6 us (22%)
  starting transfers between devices  12.4 us (9%)
  local copies, waits for them, and re-layouts  9.06 us (7%)
  between operations  1.8 us (1%)
    unnamed x1, blocking collectives  40.9 us
    pmax x1, blocking collectives, shards(): global_max = lax.pmax(local_max, ('gx', 'gy', 'gz'))  40.1 us
    ppermute x3, starting transfers between devices, padded(): after = lax.ppermute(leading, axis, down)  9.55 us
    unnamed x25, other arithmetic  8 us
    add x5, other arithmetic, invert(): first[other] = sine * first_p + cosine * first_q  4.27 us
    slice x4, local copies, waits for them, and re-layouts, padded(): last = lax.slice_in_dim(shard, length - width, length, axis=dim)  3.34 us
    ppermute x3, starting transfers between devices, padded(): before = lax.ppermute(last, axis, up)  2.86 us
    add x5, other arithmetic, invert(): table[entry_key(rest, other)] = sine * near + cosine * far  2.86 us
  transfers between devices with their start and end apart: 6, of which 0 were waited for; matrix products, arithmetic and copies ran while one was open for 11% of the time, Pallas kernels for 0%

profile of v1, /device:TPU:10, one launch (start us, length us, event | category | flops | bytes accessed | tf_op | source)
XLA Modules:
  0.0 132.8 jit_solution(7753417222536576965)
XLA Ops:
  0.6 1.1 subtract_subtract_fusion.4
  1.8 1.5 %divide_sqrt_fusion = (f32[1,4,16,512]{3,2,1,0:T(8,128)S(1)}, f32[1,4,16,512]{3,2,1,0:T(8,128)S(1)}, f32[1,4,16,512]{3,2,1,0:T(8,128)S(1)}, f32[1,4,16,512]{3,2,...) fusion(f32[8,4,16,512]{3,2,1,0:T(8,128)} %param.3, ...), kind=kLoop, calls=%fused_computation.610 | loop fusion | flops 1179648 | bytes 2228224 | tf_op jit(solution)/shard_map/sqrt | solution.py:53
  3.5 1.1 multiply_add_fusion.28
  4.6 0.4 multiply_subtract_fusion.86
  5.0 0.5 multiply_add_fusion.83
  5.5 0.9 multiply_add_fusion.23
  6.4 0.3 multiply_add_fusion.76
  6.7 0.3 fusion.211
  7.1 1.1 multiply_add_fusion.16
  8.2 0.8 multiply_subtract_fusion.105
  9.2 0.8 multiply_add_fusion.11
  10.0 0.3 multiply_subtract_fusion.50
  10.3 0.8 multiply_add_fusion.44
  11.1 1.1 multiply_add_fusion.36
  12.1 0.3 multiply_add_fusion.4
  12.5 0.3 fusion.171
  12.8 0.6 multiply_multiply_fusion
  13.8 0.7 constant_dynamic-update-slice_fusion.18
  14.4 0.7 constant_dynamic-update-slice_fusion.17
  15.5 0.8 copy-done.4
  16.4 0.7 slice_bitcast_fusion.25
  17.1 0.3 copy-done.5
  17.4 0.8 slice_bitcast_fusion.24
  18.2 0.9 fusion.284
  19.1 1.7 %collective-permute-start.1 = (f32[10,1,16,512]{3,2,1,0:T(8,128)}, f32[10,1,16,512]{3,2,1,0:T(8,128)S(1)}, u32[]{:S(2)}, u32[]{:S(2)}) collective-permute-start(f32[10,1,16,512]{3,2,1,0:T(8,128)} %get-tuple-element.278), channel_id=1, source_target_pairs={{8,0},{16,8},{24,16},{0,24},{9,1},{17,9},{25,17},{1,25},{10,2},{18... | collective-permute-start | bytes 983048 | tf_op jit(solution)/shard_map/ppermute | solution.py:20
  20.9 0.8 fusion.285
  21.7 0.7 copy.31
  22.3 1.6 %collective-permute-start.2 = (f32[10,4,1,512]{3,0,2,1:T(8,128)}, f32[10,4,1,512]{3,0,2,1:T(8,128)}, u32[]{:S(2)}, u32[]{:S(2)}) collective-permute-start(f32[10,4,1,512]{3,0,2,1:T(8,128)} %copy.31), channel_id=1, source_target_pairs={{0,2},{2,4},{4,6},{6,0},{1,3},{3,5},{5,7},{7,1},{8,10},{10,12},{12... | collective-permute-start | bytes 245768 | tf_op jit(solution)/shard_map/ppermute | solution.py:19
  23.9 0.9 fusion.286
  24.9 1.3 collective-permute-start.4
  26.1 6.0 %collective-permute-start.5 = (f32[10,4,16,1]{3,2,1,0:T(8,128)}, f32[10,4,16,1]{3,2,1,0:T(8,128)}, u32[]{:S(2)}, u32[]{:S(2)}) collective-permute-start(f32[10,4,16,1]{3,2,1,0:T(8,128)} %get-tuple-element.282), channel_id=1, source_target_pairs={{1,0},{3,2},{5,4},{7,6},{9,8},{11,10},{13,12},{15,14},{17,16},{19,... | collective-permute-start | bytes 7688 | tf_op jit(solution)/shard_map/ppermute | solution.py:20
  32.1 1.4 %abs_reduce_fusion.1 = (f32[4,16,512]{2,1,0:T(8,128)S(1)}, f32[4,16,512]{2,1,0:T(8,128)S(1)}, f32[4,16,512]{2,1,0:T(8,128)S(1)}) fusion(f32[4,16,512]{2,1,0:T(8,128)} %get-tuple-element.293, f32[4,16,512]{2,1,0:T(8,128)} %get-tuple-element.287, f32[1,4,16,512]{3,2,1,0:T(8,128)S(1)} %get-tuple-element.61, f32[1,4,16,512]{3,2,1,0:T(8,128)} %get-tuple-element.63, ...), kind=kLoop, calls=%fused_computation.48 | loop fusion | flops 1867776 | bytes 1703936 | tf_op jit(solution)/shard_map/reduce_max | solution.py:145
  33.5 0.6 add_reduce_fusion
  34.2 40.1 %pmax.7 = f32[]{:T(128)} all-reduce(f32[]{:T(128)} %add_reduce_fusion), channel_id=1, replica_groups=mesh['gx'=4,'gy'=4,'gz'=2] {'gx','gy','gz'}, use_global_device_ids=true, to_apply=%region_4.5 | all-reduce | flops 1 | bytes 8 | tf_op jit(solution)/shard_map/pmax | solution.py:149
  74.2 0.9 copy.32
  75.9 1.8 %collective-permute-start.3 = (f32[10,4,1,512]{3,0,2,1:T(8,128)S(1)}, f32[10,4,1,512]{3,0,2,1:T(8,128)S(1)}, u32[]{:S(2)}, u32[]{:S(2)}) collective-permute-start(f32[10,4,1,512]{3,0,2,1:T(8,128)S(1)} %copy.32), channel_id=1, source_target_pairs={{2,0},{4,2},{6,4},{0,6},{3,1},{5,3},{7,5},{1,7},{10,8},{12,10},{14... | collective-permute-start | bytes 245768 | tf_op jit(solution)/shard_map/ppermute | solution.py:20
  77.7 2.0 %pad_maximum_fusion.1 = f32[10,4,16,514]{3,2,1,0:T(8,128)S(1)} fusion(f32[10,4,16,1]{3,2,1,0:T(8,128)} %collective-permute-done.5, f32[10,4,16,512]{3,2,1,0:T(8,128)} %copy-done.1, f32[10,4,16,1]{3,2,1,0:T(8,128)} %collective-permute-done.4), kind=kLoop, calls=%fused_computation.37 | loop fusion | flops 657920 | bytes 2631680 | tf_op jit(solution)/shard_map/concatenate | solution.py:21
  79.9 0.5 bitcast_dynamic-update-slice_fusion.15
  80.6 0.2 bitcast_dynamic-update-slice_fusion.13
  80.9 0.3 bitcast_dynamic-update-slice_fusion.12
  81.4 0.2 bitcast_dynamic-update-slice_fusion.10
  81.7 0.2 bitcast_dynamic-update-slice_fusion.9
  81.9 0.3 bitcast_dynamic-update-slice_fusion.8
  82.4 1.1 copy.33
  83.6 0.4 pad_maximum_fusion
  84.2 0.5 bitcast_dynamic-update-slice_fusion.7
  84.7 0.3 bitcast_dynamic-update-slice_fusion.6
  84.9 0.3 bitcast_dynamic-update-slice_fusion.5
  85.2 0.4 bitcast_dynamic-update-slice_fusion.4
  85.6 0.3 bitcast_dynamic-update-slice_fusion.3
  85.9 0.3 bitcast_dynamic-update-slice_fusion.2
  86.2 0.3 bitcast_dynamic-update-slice_fusion.1
  86.5 0.3 bitcast_dynamic-update-slice_fusion
  86.9 0.3 add_dynamic-update-slice_fusion.7
  87.3 0.3 add_dynamic-update-slice_fusion.6
  87.6 0.3 add_dynamic-update-slice_fusion.5
  87.9 0.3 add_dynamic-update-slice_fusion.4
  88.2 0.3 add_dynamic-update-slice_fusion.3
  88.5 0.3 add_dynamic-update-slice_fusion.2
  88.8 0.3 add_dynamic-update-slice_fusion.1
  89.2 0.3 add_dynamic-update-slice_fusion
  89.5 1.6 %fusion.223 = (f32[8]{0:T(128)S(1)}, f32[8,4,16,512]{3,2,1,0:T(8,128)}) fusion(f32[8,4,16,512]{3,2,1,0:T(8,128)S(1)} %copy-done, f32[8,4,16,513]{3,2,1,0:T(8,128)S(1)} %broadcast_select_fusion, f32[8,4,17,512]{3,2,1,0:T(8,128)S(1)} %bitcast_dynamic-update-slice_fusion, f32[8,5,16,512]{3,2,1,0:T(8,128)S(1)} %add_dynamic-update-slice_fusion, f32[]{:T(128)S(6)} %div.553), kind=kLoop, calls=%fused_computation.747 | loop fusion | flops 2097144 | bytes 8388644 | tf_op jit(solution)/shard_map/reduce_sum | solution.py:152
  91.3 40.9 %all-reduce = f32[256]{0:T(256)S(1)} all-reduce(f32[256]{0:T(256)S(1)} %dynamic-update-slice), channel_id=2, replica_groups=mesh['gx'=4,'gy'=4,'gz'=2] {'gx','gy','gz'}, use_global_device_ids=true, to_apply=%add | all-reduce | flops 256 | bytes 2048
  132.3 0.5 broadcast_multiply_fusion
  (42 shorter events, 2.5 us)
Async XLA Ops:
  1.8 1.7 %copy-start = (f32[8,4,16,512]{3,2,1,0:T(8,128)S(1)}, f32[8,4,16,512]{3,2,1,0:T(8,128)}, u32[]{:S(2)}) copy-start(f32[8,4,16,512]{3,2,1,0:T(8,128)} %param.3) | copy-start | bytes 3145732
  15.4 1.0 copy-start.4
  16.4 1.0 copy-start.5
  18.2 6.7 %copy-start.1 = (f32[10,4,16,512]{3,2,1,0:T(8,128)}, f32[10,4,16,512]{3,2,1,0:T(8,128)S(1)}, u32[]{:S(2)}) copy-start(f32[10,4,16,512]{3,2,1,0:T(8,128)S(1)} %get-tuple-element.291) | copy-start | bytes 3932164
  18.2 6.7 %copy-start.2 = (f32[10,4,16,512]{3,2,1,0:T(8,128)}, f32[10,4,16,512]{3,2,1,0:T(8,128)S(1)}, u32[]{:S(2)}) copy-start(f32[10,4,16,512]{3,2,1,0:T(8,128)S(1)} %get-tuple-element.290) | copy-start | bytes 3932164
  19.1 67.7 %collective-permute-start = (f32[10,1,16,512]{3,2,1,0:T(8,128)}, f32[10,1,16,512]{3,2,1,0:T(8,128)S(1)}, u32[]{:S(2)}, u32[]{:S(2)}) collective-permute-start(f32[10,1,16,512]{3,2,1,0:T(8,128)} %get-tuple-element.277), channel_id=1, source_target_pairs={{0,8},{8,16},{16,24},{24,0},{1,9},{9,17},{17,25},{25,1},{2,10},{10... | collective-permute-start | bytes 983048 | tf_op jit(solution)/shard_map/ppermute | solution.py:19
  19.1 67.7 %collective-permute-start.1 = (f32[10,1,16,512]{3,2,1,0:T(8,128)}, f32[10,1,16,512]{3,2,1,0:T(8,128)S(1)}, u32[]{:S(2)}, u32[]{:S(2)}) collective-permute-start(f32[10,1,16,512]{3,2,1,0:T(8,128)} %get-tuple-element.278), channel_id=1, source_target_pairs={{8,0},{16,8},{24,16},{0,24},{9,1},{17,9},{25,17},{1,25},{10,2},{18... | collective-permute-start | bytes 983048 | tf_op jit(solution)/shard_map/ppermute | solution.py:20
  22.3 60.0 %collective-permute-start.2 = (f32[10,4,1,512]{3,0,2,1:T(8,128)}, f32[10,4,1,512]{3,0,2,1:T(8,128)}, u32[]{:S(2)}, u32[]{:S(2)}) collective-permute-start(f32[10,4,1,512]{3,0,2,1:T(8,128)} %copy.31), channel_id=1, source_target_pairs={{0,2},{2,4},{4,6},{6,0},{1,3},{3,5},{5,7},{7,1},{8,10},{10,12},{12... | collective-permute-start | bytes 245768 | tf_op jit(solution)/shard_map/ppermute | solution.py:19
  24.9 51.0 %collective-permute-start.4 = (f32[10,4,16,1]{3,2,1,0:T(8,128)}, f32[10,4,16,1]{3,2,1,0:T(8,128)}, u32[]{:S(2)}, u32[]{:S(2)}) collective-permute-start(f32[10,4,16,1]{3,2,1,0:T(8,128)} %get-tuple-element.281), channel_id=1, source_target_pairs={{0,1},{2,3},{4,5},{6,7},{8,9},{10,11},{12,13},{14,15},{16,17},{18,... | collective-permute-start | bytes 7688 | tf_op jit(solution)/shard_map/ppermute | solution.py:19
  26.1 51.6 %collective-permute-start.5 = (f32[10,4,16,1]{3,2,1,0:T(8,128)}, f32[10,4,16,1]{3,2,1,0:T(8,128)}, u32[]{:S(2)}, u32[]{:S(2)}) collective-permute-start(f32[10,4,16,1]{3,2,1,0:T(8,128)} %get-tuple-element.282), channel_id=1, source_target_pairs={{1,0},{3,2},{5,4},{7,6},{9,8},{11,10},{13,12},{15,14},{17,16},{19,... | collective-permute-start | bytes 7688 | tf_op jit(solution)/shard_map/ppermute | solution.py:20
  75.9 7.6 %collective-permute-start.3 = (f32[10,4,1,512]{3,0,2,1:T(8,128)S(1)}, f32[10,4,1,512]{3,0,2,1:T(8,128)S(1)}, u32[]{:S(2)}, u32[]{:S(2)}) collective-permute-start(f32[10,4,1,512]{3,0,2,1:T(8,128)S(1)} %copy.32), channel_id=1, source_target_pairs={{2,0},{4,2},{6,4},{0,6},{3,1},{5,3},{7,5},{1,7},{10,8},{12,10},{14... | collective-permute-start | bytes 245768 | tf_op jit(solution)/shard_map/ppermute | solution.py:20
  82.2 1.4 %copy-start.3 = (f32[10,4,16,512]{3,2,1,0:T(8,128)S(1)}, f32[10,4,16,512]{3,2,1,0:T(8,128)}, u32[]{:S(2)}) copy-start(f32[10,4,16,512]{3,2,1,0:T(8,128)} %copy-done.2) | copy-start | bytes 3932164
